TPU v7x, 32 devices: a whole 2x2x4 slice. The times are simulated.
32 devices in a mesh: pipe: 4 (over y, core), vocab: 2 (over x), expert: 4 (over z).
Axes of the slice: x: 2, y: 2, z: 4, core: 2. Of those that a mesh axis runs over, the one named last changes fastest.
Arguments:
- token_ids: int32 [192], replicated, may hold values from 0 to 65535
- routes: int32 [192, 2], replicated, may hold values from 0 to 3, all different within a row; in each aligned block of 192 rows (0 to 191, 192 to 383, ...) at most 144 rows name the same one
- gate_weights: float32 [192, 2], replicated, may hold values from 0.2 to 1
- embed_table: bfloat16 [65536, 7168], P(('pipe', 'vocab'), 'expert'), may hold values from -0.59765625 to 0.59765625
- w_gate: bfloat16 [4, 7168, 2048], P('expert', None, ('pipe', 'vocab')), may hold values from -0.5 to 0.5
- w_up: bfloat16 [4, 7168, 2048], P('expert', None, ('pipe', 'vocab')), may hold values from -0.5 to 0.5
- w_down: bfloat16 [4, 2048, 7168], P('expert', ('pipe', 'vocab')), may hold values from -0.125 to 0.125
Outputs:
- logits: bfloat16 [192, 65536], P('expert', ('pipe', 'vocab'))
Inputs may be any that keep to these rules, and one draw needn't show every extreme that they name: `routes`: each row names 2 different experts; over all 192 rows no expert is named more than 144 times, a bound that some block reaches.
All inputs are finite; a program needn't handle non-finite values.
Results may differ from a plain program's by a relative error of at most 0.025.
Values may be sent and summed in bfloat16 or wider, within the bound.
A program may use at most 128 MiB of HBM per device.

v0:
```python
import jax
import jax.numpy as jnp
from jax import lax
from jax.sharding import PartitionSpec as P


def per_device(token_ids, routes, gate_weights, embed_table, w_gate, w_up, w_down):
    vocab_rows, width_cols = embed_table.shape
    tokens, top_count = routes.shape
    experts = lax.axis_size("expert")
    group_size = lax.axis_size(("pipe", "vocab"))
    capacity = group_size * (3 * tokens * top_count // (2 * experts * group_size))
    row_base = lax.axis_index(("pipe", "vocab")) * vocab_rows
    local_ids = token_ids - row_base
    in_shard = (local_ids >= 0) & (local_ids < vocab_rows)
    lookup_rows = jnp.take(embed_table, jnp.clip(local_ids, 0, vocab_rows - 1), axis=0)
    lookup_rows = jnp.where(in_shard[:, None], lookup_rows.astype(jnp.float32), 0.0)
    embedded = lax.psum(lookup_rows.astype(jnp.bfloat16), ("pipe", "vocab"))
    flat_routes = routes.reshape(-1)
    one_hot = (flat_routes[:, None] == jnp.arange(experts, dtype=jnp.int32)[None, :]).astype(
        jnp.int32
    )
    slot_index = jnp.sum((jnp.cumsum(one_hot, axis=0) - one_hot) * one_hot, axis=1)
    slot_dest = flat_routes * capacity + slot_index
    repeated = jnp.repeat(embedded, top_count, axis=0)
    buffer = jnp.zeros((experts * capacity, width_cols), jnp.bfloat16).at[slot_dest].set(repeated)
    buffer = buffer.reshape(experts, capacity, width_cols)
    flat_rows = lax.all_to_all(buffer, "expert", split_axis=0, concat_axis=2, tiled=True)[0]
    gate_proj = jnp.dot(flat_rows, w_gate[0], preferred_element_type=jnp.float32)
    up_proj = jnp.dot(flat_rows, w_up[0], preferred_element_type=jnp.float32)
    hidden = (jax.nn.silu(gate_proj) * up_proj).astype(jnp.bfloat16)
    partial_value = jnp.dot(hidden, w_down[0], preferred_element_type=jnp.float32)[None]
    shared = lax.psum_scatter(
        partial_value.astype(jnp.bfloat16), ("pipe", "vocab"), scatter_dimension=1, tiled=True
    ).astype(jnp.float32)
    shared = lax.all_to_all(
        shared.astype(jnp.bfloat16), "expert", split_axis=2, concat_axis=0, tiled=True
    ).astype(shared.dtype)
    returned = lax.all_gather(
        shared.astype(jnp.bfloat16), ("pipe", "vocab"), axis=1, tiled=True
    ).astype(shared.dtype)
    picked = returned.reshape(experts * capacity, width_cols)[slot_dest].reshape(
        tokens, top_count, width_cols
    )
    moe_out = jnp.sum(picked * gate_weights[:, :, None], axis=1)
    residual = (embedded.astype(jnp.float32) + moe_out).astype(jnp.bfloat16)
    return lax.psum_scatter(
        lax.dot_general(
            residual, embed_table, (((1,), (1,)), ((), ())), preferred_element_type=jnp.float32
        ).astype(jnp.bfloat16),
        "expert",
        scatter_dimension=0,
        tiled=True,
    )


def solution(mesh):
    return jax.shard_map(
        per_device,
        mesh=mesh,
        in_specs=(
            P(),
            P(),
            P(),
            P(("pipe", "vocab"), "expert"),
            P("expert", None, ("pipe", "vocab")),
            P("expert", None, ("pipe", "vocab")),
            P("expert", ("pipe", "vocab"), None),
        ),
        out_specs=P("expert", ("pipe", "vocab")),
        check_vma=False,
    )
```

profile of v0, /device:TPU:0, one launch (start us, length us, event | category | flops | bytes accessed | tf_op | source)
XLA Modules:
  0.0 428.2 jit_solution(8567750402209135640)
XLA Ops:
  6.5 0.0 all-reduce.4.cloned.1.call-start
  6.5 0.7 compare_and_fusion
  7.2 14.9 %gather_fusion = bf16[192,1792]{1,0:T(8,128)(2,1)S(1)} fusion(bf16[8192,1792]{1,0:T(8,128)(2,1)} %param.10, s32[1024]{0:T(1024)S(1)} %pad_clamp_fusion.1), kind=kCustom, calls=%fused_computation | custom fusion | bytes 1377024 | tf_op jit(solution)/shard_map/jit(_take)/gather | solution.py:16
  22.1 0.0 copy-start.2
  22.1 1.2 select_convert_fusion
  23.3 0.0 all-reduce.4.cloned.1.call-update
  23.3 0.0 all-gather.3.cloned.1.call-start
  23.4 0.0 copy-done.2
  23.4 0.1 copy.39
  23.5 0.1 eq.29
  23.7 0.1 eq.25
  23.8 1.2 reduce-window.6
  25.1 0.2 slice_reduce_fusion
  25.3 0.2 reduce-window.9
  25.5 0.1 copy.38
  25.6 0.1 mul.44
  25.7 0.1 add_bitcast_fusion
  25.9 55.8 %all-reduce.4.cloned.1.call-done = bf16[192,1792]{1,0:T(8,128)(2,1)} async-done(((bf16[192,1792]{1,0:T(8,128)(2,1)}), bf16[192,1792]{1,0:T(8,128)(2,1)}) %all-reduce.4.cloned.1.call-update) | async-done | bytes 688144 | tf_op jit(solution)/shard_map/psum | solution.py:18
  81.6 1.8 broadcast_in_dim.42
  83.4 0.6 reshape.98
  84.0 3.3 scatter_custom_fusion
  87.3 51.2 %all_to_all.33 = bf16[4,144,1792]{2,1,0:T(8,128)(2,1)S(1)} all-to-all(bf16[4,144,1792]{2,1,0:T(8,128)(2,1)S(1)} %bitcast.66), channel_id=1, replica_groups=mesh['pipe'=4,'vocab'=2,'expert'=4] {'expert'}, dimensions={0} | all-to-all | bytes 4128768 | tf_op jit(solution)/shard_map/all_to_all | solution.py:28
  138.5 1.1 copy.41
  139.5 0.0 copy-start
  139.6 0.3 copy.50
  139.8 1.8 copy-done
  141.6 0.8 fusion.5
  142.4 6.9 %fusion.1 = bf16[1,144,7168]{2,1,0:T(8,128)(2,1)} fusion(bf16[1,256,7168]{2,1,0:T(8,128)(2,1)} %param.13, bf16[144,7168]{1,0:T(8,128)(2,1)S(1)} %bitcast.63, bf16[1,7168,256]{2,1,0:T(8,128)(2,1)} %param.12, f32[144,256]{1,0:T(8,128)S(1)} %fusion.5), kind=kOutput, calls=%fused_computation.5 | convolution fusion | flops 1058217984 | bytes 11616256 | tf_op jit(solution)/shard_map/dot_general | solution.py:32
  149.2 0.0 copy-start.4
  149.2 58.3 %fusion = bf16[24,7168]{1,0:T(8,128)(2,1)S(1)} fusion(bf16[1,144,7168]{2,1,0:T(8,128)(2,1)} %fusion.1), kind=kCustom, calls=%all-reduce-scatter | all-reduce-scatter fusion | flops 1376257 | bytes 2408960
  207.6 1.9 collective-permute-start
  209.5 0.1 slice.13
  209.6 1.7 collective-permute-start.1
  211.3 0.0 copy-done.4
  211.3 0.6 dynamic-slice.4
  212.6 0.0 collective-permute-done.1
  212.6 4.5 %collective-permute-done = bf16[24,7168]{1,0:T(8,128)(2,1)S(1)} collective-permute-done((bf16[24,7168]{1,0:T(8,128)(2,1)S(1)}, bf16[24,7168]{1,0:T(8,128)(2,1)S(1)}, u32[]{:S(2)}, u32[]{:S(2)}) %collective-permute-start) | collective-permute-done | bytes 344096
  217.0 4.8 %concatenate = bf16[66,7168]{1,0:T(8,128)(2,1)S(1)} concatenate(bf16[18,7168]{1,0:T(8,128)(2,1)S(1)} %collective-permute-done.1, bf16[24,7168]{1,0:T(8,128)(2,1)S(1)} %collective-permute-done, bf16[24,7168]{1,0:T(8,128)(2,1)S(1)} %fusion), dimensions={0} | concatenate | bytes 1892352
  221.9 0.1 dynamic-slice_bitcast_fusion
  222.0 6.0 %copy.42 = bf16[1,18,7168]{1,0,2:T(2,128)(2,1)} copy(bf16[1,18,7168]{2,1,0:T(8,128)(2,1)S(1)} %dynamic-slice_bitcast_fusion) | data formatting | bytes 516096 | tf_op jit(solution)/shard_map/reduce_scatter | solution.py:33
  228.0 0.5 broadcast.68
  228.5 39.8 %reduce.4 = bf16[7168,18]{1,0:T(8,128)(2,1)S(1)} reduce(bf16[7168,1,18]{2,1,0:T(2,128)(2,1)} %bitcast.64, bf16[]{:T(256)} %broadcast.68), dimensions={1}, to_apply=%bitcast.56.reduce_sub_computation | reduce | bytes 516098
  268.3 3.4 reshape.114
  271.7 9.8 %all_to_all.34 = bf16[4,2,16128]{2,1,0:T(2,128)(2,1)S(1)} all-to-all(bf16[4,2,16128]{2,1,0:T(2,128)(2,1)S(1)} %reshape.114), channel_id=1, replica_groups=mesh['pipe'=4,'vocab'=2,'expert'=4] {'expert'}, dimensions={0} | all-to-all | bytes 516096 | tf_op jit(solution)/shard_map/all_to_all | solution.py:36
  281.4 5.2 %reshape.115 = bf16[7168,1,18]{2,1,0:T(2,128)(2,1)} reshape(bf16[4,2,16128]{2,1,0:T(2,128)(2,1)S(1)} %all_to_all.34) | data formatting | bytes 516096
  286.6 0.0 copy-start.3
  286.6 7.3 %copy.43 = bf16[1,18,7168]{2,1,0:T(8,128)(2,1)S(1)} copy(bf16[1,18,7168]{1,0,2:T(2,128)(2,1)} %bitcast.65) | data formatting | bytes 516096 | tf_op jit(solution)/shard_map/all_to_all | solution.py:36
  293.9 0.8 all_to_all.28
  294.7 0.0 all-gather.3.cloned.1.call-update
  294.7 0.3 reduce-scatter.5.cloned.1.call-start
  295.0 0.0 copy-done.3
  295.0 0.1 copy.46
  295.1 29.7 %all-gather.3.cloned.1.call-done = bf16[4,1,144,1792]{3,0,1,2:T(4,128)(2,1)} async-done(((bf16[4,1,18,1792]{3,0,1,2:T(4,128)(2,1)}), bf16[4,1,144,1792]{3,0,1,2:T(4,128)(2,1)}) %all-gather.3.cloned.1.call-update) | async-done | bytes 2064400 | tf_op jit(solution)/shard_map/all_gather | solution.py:39
  324.8 1.8 copy.45
  326.6 2.4 bitcast_convert_fusion
  329.0 6.1 %gather_fusion.1 = f32[384,1792]{1,0:T(8,128)S(1)} fusion(f32[576,1792]{1,0:T(8,128)} %bitcast_convert_fusion, s32[1024]{0:T(1024)S(1)} %pad_clamp_fusion), kind=kCustom, calls=%fused_computation.1 | custom fusion | bytes 5506560 | tf_op jit(solution)/shard_map/gather | solution.py:42
  335.1 2.8 reshape.75
  337.8 0.0 copy-start.1
  337.8 5.9 %multiply_reduce_fusion = f32[192,1792]{1,0:T(8,128)S(1)} fusion(f32[192,2,1792]{2,1,0:T(2,128)} %reshape.75, f32[192,2]{1,0:T(8,128)S(1)} %copy.46), kind=kLoop, calls=%fused_computation.11 | loop fusion | flops 1032192 | bytes 4130304 | tf_op jit(solution)/shard_map/reduce_sum | solution.py:45
  343.7 0.0 copy-done.1
  343.8 17.4 %convolution_convert_fusion = bf16[192,8192]{1,0:T(8,128)(2,1)} fusion(bf16[8192,1792]{1,0:T(8,128)(2,1)} %param.10, f32[192,1792]{1,0:T(8,128)S(1)} %multiply_reduce_fusion, bf16[192,1792]{1,0:T(8,128)(2,1)S(1)} %copy-done.1), kind=kOutput, calls=%fused_computation.3 | convolution fusion | flops 5639749632 | bytes 34570240 | tf_op jit(solution)/shard_map/dot_general | solution.py:48
  361.1 0.0 reduce-scatter.5.cloned.1.call-update
  361.1 60.6 %reduce-scatter.5.cloned.1.call-done = bf16[48,8192]{1,0:T(8,128)(2,1)} async-done(((bf16[192,8192]{1,0:T(8,128)(2,1)}), bf16[48,8192]{1,0:T(8,128)(2,1)}) %reduce-scatter.5.cloned.1.call-update) | async-done | bytes 786448 | tf_op jit(solution)/shard_map/reduce_scatter | solution.py:47
  (6 shorter events, 0.1 us)
Async XLA Ops:
  6.5 75.1 %all-reduce.4.cloned.1.call-start = ((), (), s32[]{:S(2)}) async-start(), calls=%async_computation.3 | async-start | bytes 1376256 | tf_op jit(solution)/shard_map/psum | solution.py:18
  22.1 1.3 copy-start.2
  23.3 301.5 %all-gather.3.cloned.1.call-start = ((), (), s32[]{:S(2)}) async-start(), calls=%async_computation.5 | async-start | bytes 2322432 | tf_op jit(solution)/shard_map/all_gather | solution.py:39
  139.5 2.0 copy-start
  149.2 62.1 %copy-start.4 = (u32[32]{0:T(128)S(1)}, u32[32]{0:T(128)}, u32[]{:S(2)}) copy-start(u32[32]{0:T(128)} %constant.54) | copy-start | bytes 388
  207.6 9.5 %collective-permute-start = (bf16[24,7168]{1,0:T(8,128)(2,1)S(1)}, bf16[24,7168]{1,0:T(8,128)(2,1)S(1)}, u32[]{:S(2)}, u32[]{:S(2)}) collective-permute-start(bf16[24,7168]{1,0:T(8,128)(2,1)S(1)} %fusion), channel_id=1, source_target_pairs={{0,4},{4,8},{8,12},{12,16},{16,20},{20,24},{24,28},{1,5},{5,9},{9,... | collective-permute-start | bytes 1032200
  209.6 3.0 collective-permute-start.1
  286.6 8.4 %copy-start.3 = (f32[192,2]{0,1:T(2,128)S(1)}, f32[192,2]{0,1:T(2,128)}, u32[]{:S(2)}) copy-start(f32[192,2]{0,1:T(2,128)} %param.9) | copy-start | bytes 4612
  294.7 127.0 %reduce-scatter.5.cloned.1.call-start = ((), (), s32[]{:S(2)}) async-start(), calls=%async_computation.4 | async-start | bytes 3932160 | tf_op jit(solution)/shard_map/reduce_scatter | solution.py:47
  337.8 5.9 %copy-start.1 = (bf16[192,1792]{1,0:T(8,128)(2,1)S(1)}, bf16[192,1792]{1,0:T(8,128)(2,1)}, u32[]{:S(2)}) copy-start(bf16[192,1792]{1,0:T(8,128)(2,1)} %all-reduce.4.cloned.1.call-done) | copy-start | bytes 2064388
Sparse Core Ops, SparseCore 0:
  23.5 58.1 all-reduce.3
  294.8 29.9 all-gather.2
  361.3 60.3 reduce-scatter.4
where the time goes:
time: 429 us; the launch traced here: 428 us
  waiting for transfers between devices  151 us (35%)
  blocking collectives  119 us (28%)
  local copies, waits for them, and re-layouts  64 us (15%)
  other arithmetic  51.5 us (12%)
  matrix products  25 us (6%)
  between operations  14 us (3%)
    reduce_scatter x1, waiting for transfers between devices, per_device(): lax.psum_scatter(lax.dot_general(residual, embed_table, (((1,), (1,)), ((...  60.6 us
    unnamed x1, blocking collectives  58.3 us
    psum x1, waiting for transfers between devices, per_device(): embedded = lax.psum(lookup_rows.astype(jnp.bfloat16), ('pipe', 'vocab'))  55.8 us
    all_to_all x1, blocking collectives, per_device(): lax.all_to_all(buffer, 'expert', split_axis=0, concat_axis=2, tiled=True)[0]  51.2 us
    unnamed x2, other arithmetic  39.8 us
    all_gather x1, waiting for transfers between devices, per_device(): lax.all_gather(shared.astype(jnp.bfloat16), ('pipe', 'vocab'), axis=1, ti...  29.7 us
    dot_general x1, matrix products, per_device(): lax.dot_general(residual, embed_table, (((1,), (1,)), ((), ())), preferre...  17.4 us
    unnamed x20, local copies, waits for them, and re-layouts  16.9 us
  transfers between devices with their start and end apart: 5, of which 4 were waited for; matrix products, arithmetic and copies ran while one was open for 1% of the time, Pallas kernels for 0%

commit v1 on v0

--- a/solution.py
+++ b/solution.py
@@ -36,8 +36,14 @@
     shared = lax.all_to_all(
         shared.astype(jnp.bfloat16), "expert", split_axis=2, concat_axis=0, tiled=True
     ).astype(shared.dtype)
-    returned = lax.all_gather(
-        shared.astype(jnp.bfloat16), ("pipe", "vocab"), axis=1, tiled=True
+    returned = jnp.concatenate(
+        lax.all_to_all(
+            jnp.stack([shared.astype(jnp.bfloat16)] * lax.axis_size(("pipe", "vocab"))),
+            ("pipe", "vocab"),
+            0,
+            0,
+        ),
+        axis=1,
     ).astype(shared.dtype)
     picked = returned.reshape(experts * capacity, width_cols)[slot_dest].reshape(
         tokens, top_count, width_cols

time: 429 us -> 454 us (1.058); the launches traced: 428 us -> 446 us
  blocking collectives: 119 us -> 130 us
  local copies, waits for them, and re-layouts: 64 us -> 71.9 us
  waiting for transfers between devices: 151 us -> 144 us
  starting transfers between devices: 3.96 us -> 10.7 us
    all_gather x1 -> x0, waiting for transfers between devices: 29.7 us -> none  [per_device(): lax.all_gather(shared.astype(jnp.bfloat16), ('pipe', 'vocab'), axis=1, ti...]
    all_to_all x0 -> x1, waiting for transfers between devices: none -> 25.3 us  [per_device(): lax.all_to_all(jnp.stack([shared.astype(jnp.bfloat16)] * lax.axis_size(('...]
    all_to_all x1, blocking collectives: 51.2 us -> 61.5 us  [per_device(): lax.all_to_all(buffer, 'expert', split_axis=0, concat_axis=2, tiled=True)[0]]
    convert_element_type x0 -> x2, local copies, waits for them, and re-layouts: none -> 8.49 us  [per_device(): returned = jnp.concatenate(lax.all_to_all(jnp.stack([shared.astype(jnp.bf...]
    all_to_all x0 -> x1, starting transfers between devices: none -> 6.8 us  [per_device(): lax.all_to_all(jnp.stack([shared.astype(jnp.bfloat16)] * lax.axis_size(('...]
where the time goes in v1:
time: 454 us; the launch traced here: 446 us
  waiting for transfers between devices  144 us (32%)
  blocking collectives  130 us (29%)
  local copies, waits for them, and re-layouts  71.9 us (16%)
  other arithmetic  49.6 us (11%)
  matrix products  25 us (6%)
  between operations  14.7 us (3%)
  starting transfers between devices  10.7 us (2%)
    all_to_all x1, blocking collectives, per_device(): lax.all_to_all(buffer, 'expert', split_axis=0, concat_axis=2, tiled=True)[0]  61.5 us
    reduce_scatter x1, waiting for transfers between devices, per_device(): lax.psum_scatter(lax.dot_general(residual, embed_table, (((1,), (1,)), ((...  58.5 us
    unnamed x1, blocking collectives  58.3 us
    psum x1, waiting for transfers between devices, per_device(): embedded = lax.psum(lookup_rows.astype(jnp.bfloat16), ('pipe', 'vocab'))  55.8 us
    unnamed x2, other arithmetic  39.8 us
    all_to_all x1, waiting for transfers between devices, per_device(): lax.all_to_all(jnp.stack([shared.astype(jnp.bfloat16)] * lax.axis_size(('...  25.3 us
    dot_general x1, matrix products, per_device(): lax.dot_general(residual, embed_table, (((1,), (1,)), ((), ())), preferre...  17.3 us
    unnamed x20, local copies, waits for them, and re-layouts  16.9 us
  transfers between devices with their start and end apart: 5, of which 4 were waited for; matrix products, arithmetic and copies ran while one was open for 1% of the time, Pallas kernels for 0%

profile of v1, /device:TPU:0, one launch (start us, length us, event | category | flops | bytes accessed | tf_op | source)
XLA Modules:
  0.0 445.6 jit_solution(3523570906340268795)
XLA Ops:
  6.5 0.0 all-reduce.4.cloned.1.call-start
  6.5 0.7 compare_and_fusion
  7.2 0.0 copy-start.2
  7.2 14.9 %gather_fusion = bf16[192,1792]{1,0:T(8,128)(2,1)S(1)} fusion(bf16[8192,1792]{1,0:T(8,128)(2,1)} %param.10, s32[1024]{0:T(1024)S(1)} %pad_clamp_fusion.1), kind=kCustom, calls=%fused_computation | custom fusion | bytes 1377024 | tf_op jit(solution)/shard_map/jit(_take)/gather | solution.py:16
  22.1 1.2 select_convert_fusion
  23.3 0.0 all-reduce.4.cloned.1.call-update
  23.4 0.0 copy-done.2
  23.4 0.1 copy.30
  23.5 0.1 eq.29
  23.6 0.1 eq.25
  23.8 1.2 reduce-window.6
  25.0 0.2 slice_reduce_fusion
  25.2 0.2 reduce-window.9
  25.4 0.1 copy.29
  25.6 0.1 mul.44
  25.7 0.1 add_bitcast_fusion
  25.8 55.8 %all-reduce.4.cloned.1.call-done = bf16[192,1792]{1,0:T(8,128)(2,1)} async-done(((bf16[192,1792]{1,0:T(8,128)(2,1)}), bf16[192,1792]{1,0:T(8,128)(2,1)}) %all-reduce.4.cloned.1.call-update) | async-done | bytes 688144 | tf_op jit(solution)/shard_map/psum | solution.py:18
  81.6 1.8 broadcast_in_dim.42
  83.5 0.6 reshape.98
  84.0 3.3 scatter_custom_fusion
  87.3 61.5 %all_to_all.35 = bf16[4,144,1792]{2,1,0:T(8,128)(2,1)S(1)} all-to-all(bf16[4,144,1792]{2,1,0:T(8,128)(2,1)S(1)} %bitcast.65), channel_id=1, replica_groups=mesh['pipe'=4,'vocab'=2,'expert'=4] {'expert'}, dimensions={0} | all-to-all | bytes 4128768 | tf_op jit(solution)/shard_map/all_to_all | solution.py:28
  148.9 1.1 copy.32
  149.9 0.0 copy-start
  149.9 0.3 copy.40
  150.2 1.8 copy-done
  152.0 0.8 fusion.5
  152.8 6.9 %fusion.1 = bf16[1,144,7168]{2,1,0:T(8,128)(2,1)} fusion(bf16[1,256,7168]{2,1,0:T(8,128)(2,1)} %param.13, bf16[144,7168]{1,0:T(8,128)(2,1)S(1)} %bitcast.62, bf16[1,7168,256]{2,1,0:T(8,128)(2,1)} %param.12, f32[144,256]{1,0:T(8,128)S(1)} %fusion.5), kind=kOutput, calls=%fused_computation.5 | convolution fusion | flops 1058217984 | bytes 11616256 | tf_op jit(solution)/shard_map/dot_general | solution.py:32
  159.6 0.0 copy-start.4
  159.6 58.3 %fusion = bf16[24,7168]{1,0:T(8,128)(2,1)S(1)} fusion(bf16[1,144,7168]{2,1,0:T(8,128)(2,1)} %fusion.1), kind=kCustom, calls=%all-reduce-scatter | all-reduce-scatter fusion | flops 1376257 | bytes 2408960
  217.9 2.0 collective-permute-start
  219.9 0.1 slice.13
  220.0 1.7 collective-permute-start.1
  221.7 0.0 copy-done.4
  221.7 0.6 dynamic-slice.4
  222.9 0.0 collective-permute-done.1
  222.9 4.5 %collective-permute-done = bf16[24,7168]{1,0:T(8,128)(2,1)S(1)} collective-permute-done((bf16[24,7168]{1,0:T(8,128)(2,1)S(1)}, bf16[24,7168]{1,0:T(8,128)(2,1)S(1)}, u32[]{:S(2)}, u32[]{:S(2)}) %collective-permute-start) | collective-permute-done | bytes 344096
  227.4 4.8 %concatenate = bf16[66,7168]{1,0:T(8,128)(2,1)S(1)} concatenate(bf16[18,7168]{1,0:T(8,128)(2,1)S(1)} %collective-permute-done.1, bf16[24,7168]{1,0:T(8,128)(2,1)S(1)} %collective-permute-done, bf16[24,7168]{1,0:T(8,128)(2,1)S(1)} %fusion), dimensions={0} | concatenate | bytes 1892352
  232.2 0.1 dynamic-slice_bitcast_fusion
  232.3 6.0 %copy.33 = bf16[1,18,7168]{1,0,2:T(2,128)(2,1)} copy(bf16[1,18,7168]{2,1,0:T(8,128)(2,1)S(1)} %dynamic-slice_bitcast_fusion) | data formatting | bytes 516096 | tf_op jit(solution)/shard_map/reduce_scatter | solution.py:33
  238.4 0.5 broadcast.69
  238.9 39.8 %reduce.4 = bf16[7168,18]{1,0:T(8,128)(2,1)S(1)} reduce(bf16[7168,1,18]{2,1,0:T(2,128)(2,1)} %bitcast.63, bf16[]{:T(256)} %broadcast.69), dimensions={1}, to_apply=%bitcast.55.reduce_sub_computation | reduce | bytes 516098
  278.7 3.4 reshape.110
  282.1 9.7 %all_to_all.36 = bf16[4,2,16128]{2,1,0:T(2,128)(2,1)S(1)} all-to-all(bf16[4,2,16128]{2,1,0:T(2,128)(2,1)S(1)} %reshape.110), channel_id=1, replica_groups=mesh['pipe'=4,'vocab'=2,'expert'=4] {'expert'}, dimensions={0} | all-to-all | bytes 516096 | tf_op jit(solution)/shard_map/all_to_all | solution.py:36
  291.8 5.2 %reshape.111 = bf16[7168,1,18]{2,1,0:T(2,128)(2,1)} reshape(bf16[4,2,16128]{2,1,0:T(2,128)(2,1)S(1)} %all_to_all.36) | data formatting | bytes 516096
  297.0 7.3 %copy.34 = bf16[1,18,7168]{2,1,0:T(8,128)(2,1)S(1)} copy(bf16[1,18,7168]{1,0,2:T(2,128)(2,1)} %bitcast.64) | data formatting | bytes 516096 | tf_op jit(solution)/shard_map/all_to_all | solution.py:36
  304.2 0.1 all_to_all.29
  304.4 0.0 copy-start.3
  304.4 1.9 stack.5
  306.2 6.8 %all-to-all-start.2 = ((bf16[8,4,18,1792]{3,1,2,0:T(4,128)(2,1)}), bf16[8,4,18,1792]{3,1,2,0:T(4,128)(2,1)S(1)}, u32[]{:S(2)}, u32[]{:S(2)}) async-start(bf16[8,4,18,1792]{3,1,2,0:T(4,128)(2,1)} %stack.5), calls=%async_computation.2 | async-start | bytes 4128768 | tf_op jit(solution)/shard_map/all_to_all | solution.py:40
  313.0 0.2 reduce-scatter.5.cloned.1.call-start
  313.3 0.0 copy-done.3
  313.3 0.1 copy.36
  313.4 25.3 %all-to-all-done.2 = bf16[8,4,18,1792]{3,1,2,0:T(4,128)(2,1)S(1)} async-done(((bf16[8,4,18,1792]{3,1,2,0:T(4,128)(2,1)}), bf16[8,4,18,1792]{3,1,2,0:T(4,128)(2,1)S(1)}, u32[]{:S(2)}, u32[]{:S(2)}) %all-to-all-start.2) | async-done | bytes 2064416 | tf_op jit(solution)/shard_map/all_to_all | solution.py:40
  338.7 0.5 convert_bitcast_fusion
  339.3 3.3 copy.35
  342.5 5.2 %reshape.77 = f32[576,1792]{1,0:T(8,128)} reshape(f32[4,8,18,1792]{3,2,1,0:T(8,128)} %copy.35) | data formatting | bytes 8257536 | tf_op jit(solution)/shard_map/convert_element_type | solution.py:47
  347.8 6.1 %gather_fusion.1 = f32[384,1792]{1,0:T(8,128)S(1)} fusion(f32[576,1792]{1,0:T(8,128)} %reshape.77, s32[1024]{0:T(1024)S(1)} %pad_clamp_fusion), kind=kCustom, calls=%fused_computation.1 | custom fusion | bytes 5506560 | tf_op jit(solution)/shard_map/gather | solution.py:48
  353.8 2.8 reshape.76
  356.6 0.0 copy-start.1
  356.6 5.9 %multiply_reduce_fusion = f32[192,1792]{1,0:T(8,128)S(1)} fusion(f32[192,2,1792]{2,1,0:T(2,128)} %reshape.76, f32[192,2]{1,0:T(8,128)S(1)} %copy.36), kind=kLoop, calls=%fused_computation.12 | loop fusion | flops 1032192 | bytes 4130304 | tf_op jit(solution)/shard_map/reduce_sum | solution.py:51
  362.5 0.0 copy-done.1
  362.5 17.3 %convolution_convert_fusion = bf16[192,8192]{1,0:T(8,128)(2,1)} fusion(bf16[8192,1792]{1,0:T(8,128)(2,1)} %param.10, f32[192,1792]{1,0:T(8,128)S(1)} %multiply_reduce_fusion, bf16[192,1792]{1,0:T(8,128)(2,1)S(1)} %copy-done.1), kind=kOutput, calls=%fused_computation.3 | convolution fusion | flops 5639749632 | bytes 34570240 | tf_op jit(solution)/shard_map/dot_general | solution.py:54
  379.9 0.0 reduce-scatter.5.cloned.1.call-update
  379.9 58.5 %reduce-scatter.5.cloned.1.call-done = bf16[48,8192]{1,0:T(8,128)(2,1)} async-done(((bf16[192,8192]{1,0:T(8,128)(2,1)}), bf16[48,8192]{1,0:T(8,128)(2,1)}) %reduce-scatter.5.cloned.1.call-update) | async-done | bytes 786448 | tf_op jit(solution)/shard_map/reduce_scatter | solution.py:53
  (6 shorter events, 0.1 us)
Async XLA Ops:
  6.5 75.1 %all-reduce.4.cloned.1.call-start = ((), (), s32[]{:S(2)}) async-start(), calls=%async_computation.4 | async-start | bytes 1376256 | tf_op jit(solution)/shard_map/psum | solution.py:18
  7.2 16.1 %copy-start.2 = (s32[192,2]{0,1:T(2,128)S(1)}, s32[192,2]{0,1:T(2,128)}, u32[]{:S(2)}) copy-start(s32[192,2]{0,1:T(2,128)} %param.8) | copy-start | bytes 4612
  149.9 2.0 copy-start
  159.6 62.1 %copy-start.4 = (u32[32]{0:T(128)S(1)}, u32[32]{0:T(128)}, u32[]{:S(2)}) copy-start(u32[32]{0:T(128)} %constant.54) | copy-start | bytes 388
  217.9 9.5 %collective-permute-start = (bf16[24,7168]{1,0:T(8,128)(2,1)S(1)}, bf16[24,7168]{1,0:T(8,128)(2,1)S(1)}, u32[]{:S(2)}, u32[]{:S(2)}) collective-permute-start(bf16[24,7168]{1,0:T(8,128)(2,1)S(1)} %fusion), channel_id=1, source_target_pairs={{0,4},{4,8},{8,12},{12,16},{16,20},{20,24},{24,28},{1,5},{5,9},{9,... | collective-permute-start | bytes 1032200
  220.0 3.0 collective-permute-start.1
  304.4 8.9 %copy-start.3 = (f32[192,2]{0,1:T(2,128)S(1)}, f32[192,2]{0,1:T(2,128)}, u32[]{:S(2)}) copy-start(f32[192,2]{0,1:T(2,128)} %param.9) | copy-start | bytes 4612
  306.2 32.5 %all-to-all-start.2 = ((bf16[8,4,18,1792]{3,1,2,0:T(4,128)(2,1)}), bf16[8,4,18,1792]{3,1,2,0:T(4,128)(2,1)S(1)}, u32[]{:S(2)}, u32[]{:S(2)}) async-start(bf16[8,4,18,1792]{3,1,2,0:T(4,128)(2,1)} %stack.5), calls=%async_computation.2 | async-start | bytes 4128768 | tf_op jit(solution)/shard_map/all_to_all | solution.py:40
  313.0 125.3 %reduce-scatter.5.cloned.1.call-start = ((), (), s32[]{:S(2)}) async-start(), calls=%async_computation.5 | async-start | bytes 3932160 | tf_op jit(solution)/shard_map/reduce_scatter | solution.py:53
  356.6 5.9 %copy-start.1 = (bf16[192,1792]{1,0:T(8,128)(2,1)S(1)}, bf16[192,1792]{1,0:T(8,128)(2,1)}, u32[]{:S(2)}) copy-start(bf16[192,1792]{1,0:T(8,128)(2,1)} %all-reduce.4.cloned.1.call-done) | copy-start | bytes 2064388
Sparse Core Ops, SparseCore 0:
  23.5 58.1 all-reduce.3
  380.0 58.3 reduce-scatter.4
